TPU v7x, 32 devices: a 4x4x1 block of a 4x4x8 slice. The times are simulated.
32 devices in a mesh: dp: 1 (over z), tp: 4 (over y), pp: 8 (over x, core).
Axes of the slice: x: 4, y: 4, z: 1, core: 2. Of those that a mesh axis runs over, the one named last changes fastest.
The devices are a block of a 4x4x8 slice.
Arguments:
- x_in: bfloat16 [4, 1, 1024, 1024], P('dp')
- seq_lens: int32 [4, 1], P('dp')
- ln1_gain: bfloat16 [8, 1024], P('pp')
- ln1_shift: bfloat16 [8, 1024], P('pp')
- w_qkv: bfloat16 [8, 1024, 3, 1024], P('pp', None, None, 'tp')
- b_qkv: bfloat16 [8, 3, 16, 64], P('pp', None, 'tp')
- w_out: bfloat16 [8, 1024, 1024], P('pp', 'tp')
- b_out: bfloat16 [8, 1024], P('pp')
- ln2_gain: bfloat16 [8, 1024], P('pp')
- ln2_shift: bfloat16 [8, 1024], P('pp')
- w_up: bfloat16 [8, 1024, 4096], P('pp', None, 'tp')
- b_up: bfloat16 [8, 4096], P('pp', 'tp')
- w_down: bfloat16 [8, 4096, 1024], P('pp', 'tp')
- b_down: bfloat16 [8, 1024], P('pp')
Outputs:
- output: bfloat16 [8, 4, 1, 1024, 1024], P('pp', 'dp')
All inputs are finite; a program needn't handle non-finite values.
Results may differ from a plain program's by a relative error of at most 0.02.
Values are sent between devices in bfloat16 or wider.
A program may use at most 768 MiB of HBM per device.

v0:
```python
import functools
import math

import jax
import jax.numpy as jnp
import numpy as np
from jax import lax
from jax.experimental import pallas as pl
from jax.experimental.pallas import tpu as pltpu
from jax.sharding import PartitionSpec as P

MESH = pl.DeviceIdType.MESH
UNIT = 128
LANE = 128
KBLK = 256
NEG = -1e30


def alibi_slopes(heads_n):
    closest = 2 ** int(math.floor(math.log2(heads_n)))
    base_rate = 2.0 ** (-8.0 / closest)
    slope_list = [base_rate ** (head_idx + 1) for head_idx in range(closest)]
    extra_rate = 2.0 ** (-4.0 / closest)
    slope_list = slope_list + [extra_rate ** (2 * head_idx + 1) for head_idx in range(min(closest, heads_n - closest))]
    return np.array(slope_list, dtype=np.float32)


def split_bf16(value):
    parts = []
    rest = np.float32(value)
    for _ in range(3):
        part = rest.astype(jnp.bfloat16).astype(np.float32)
        parts.append(float(part))
        rest = np.float32(rest - part)
    return parts


def layer_norm(x, gain, shift):
    mean = jnp.mean(x, axis=-1, keepdims=True)
    cent = x - mean
    var = jnp.mean(cent * cent, axis=-1, keepdims=True)
    return (cent * lax.rsqrt(var + 1e-5) * gain + shift).astype(jnp.bfloat16)


def gelu(x):
    inner = math.sqrt(2.0 / math.pi) * (x + 0.044715 * (x * x * x))
    return 0.5 * x * (1.0 + jnp.tanh(inner))


def kernel(heads_n, x_hbm, lens, wqkv_in, wout_in, wup_in, wdn_in,
           ln1_gain, ln1_shift, b_out, ln2_gain, ln2_shift, b_down, b_up, b_qkv, out,
           wqkv, wout, wup, wdn, packs, pack_in, rl_qkv, rl_out, rl_up, rl_dn, sw_qkv, sw_out, sw_up, sw_dn, sw_pack,
           xbuf, ybuf, kc0, kc1, kc2, kc3, vt0, vt1, vt2, vt3, kx, qaug, cmask, sbuf, abuf, ctx, hbuf, ubuf,
           sw_send, sw_recv, w_recv, fwd_send, rl_send, rl_recv, dir_send, pk_send, go,
           x0_sem, x_recv, s_send, od_send, da_send, db_send, fa_send, fb_send, fc_send,
           rr_recv, rr_send, o_recv):
    tp_n = 4
    units = xbuf.shape[0]
    model = xbuf.shape[2]
    seq = units * UNIT
    quarter = wqkv.shape[1] // 3 * LANE
    hid_q = wup.shape[1] * LANE
    pairs = model // LANE
    per_q = quarter // LANE

    r = lax.axis_index("tp")
    p = lax.axis_index("pp")
    x = p // 2
    c = p % 2
    odd = (r + (x + 1) // 2 + 1) % 2
    even_col = x + (1 - x % 2) * (2 - 2 * x)
    layer = odd * (2 * x + 1) + (1 - odd) * 2 * even_col
    home = odd == c
    moved = jnp.logical_and(c == 0, x % 2 == 0)
    level = x == 1
    ahead = jnp.logical_or(r % 2 == 0, level)
    rp, rm, ro = (r + 1) % tp_n, (r + 3) % tp_n, (r + 2) % tp_n
    partner = 2 * x + (1 - c)
    sig = 1 - 2 * c
    r_fwd = (r + sig + tp_n) % tp_n
    r_bwd = (r - sig + tp_n) % tp_n
    stage0, stage1 = 2 * x, 2 * x + 1
    x_n = 4

    def micro_of(row, core, lay):
        hops = (lay + 1) // 4
        return 2 * (((row + 8 - (1 - 2 * core) * hops) % tp_n) // 2) + core

    m = micro_of(r, c, layer)

    def rcopy(src, dst, ssem, rsem, **dev):
        return pltpu.make_async_remote_copy(src_ref=src, dst_ref=dst, send_sem=ssem, recv_sem=rsem,
                                            device_id=dev, device_id_type=MESH)

    barrier = pltpu.get_barrier_semaphore()
    for dr in range(tp_n):
        for dc in range(2):
            if dr or dc:
                pl.semaphore_signal(barrier, inc=1, device_id={"tp": (r + dr) % tp_n, "pp": 2 * x + (c + dc) % 2}, device_id_type=MESH)
    for dx in range(1, x_n):
        pl.semaphore_signal(barrier, inc=1, device_id={"pp": 2 * ((x + dx) % x_n) + c}, device_id_type=MESH)

    for i, vec in enumerate((ln1_gain, ln1_shift, b_out, ln2_gain, ln2_shift, b_down, b_up)):
        pack_in[i:i + 1, :] = vec[...].astype(jnp.float32)
    width = b_qkv.shape[3]
    for j in range(3):
        for head in range(quarter // width):
            at = j * quarter + head * width
            pack_in[7:8, at:at + width] = b_qkv[0, j, head:head + 1, :].astype(jnp.float32)
    pl.semaphore_wait(barrier, 10)

    def wsrc(k, h, n):
        if k == 0:
            return wqkv_in.at[n // per_q, pl.ds(h * (model // 2), model // 2), pl.ds(n % per_q * LANE, LANE)]
        ref = (None, wout_in, wup_in, wdn_in)[k]
        half = ref.shape[0] // 2
        return ref.at[pl.ds(h * half, half), pl.ds(n * LANE, LANE)]

    def wdst(k, q, h=0):
        if k == 4:
            return packs.at[q]
        if k == 0 or k == 2:
            return (wqkv, None, wup)[k].at[q, :, pl.ds(h * (model // 2), model // 2), :]
        ref, half = (wout, quarter // 2) if k == 1 else (wdn, hid_q // 2)
        return ref.at[:, pl.ds(pl.multiple_of((2 * q + h) * half, half), half), :]

    def rl(k, h):
        return (rl_qkv, rl_out, rl_up, rl_dn)[k].at[h]

    def sw(k, h):
        if k == 4:
            return sw_pack
        ref = (sw_qkv, sw_out, sw_up, sw_dn)[k]
        half = ref.shape[1] // 2
        return ref.at[:, pl.ds(h * half, half), :]

    def fetch(k, h, dst, move):
        if k == 4:
            todo = [(pack_in, dst)]
        else:
            todo = [(wsrc(k, h, n), dst.at[n]) for n in range(dst.shape[0])]
        for src, to in todo:
            if move:
                rcopy(src, to, sw_send.at[k, h], sw_recv.at[k, h], pp=2 * (2 - x)).start()
            else:
                pltpu.make_async_copy(src, to, sw_recv.at[k, h]).start()

    def wwait(view, sem):
        rcopy(view, view, sem, sem, pp=partner).wait_recv()

    pieces = [(4, 0), (1, 0), (1, 1), (0, 0), (0, 1), (2, 0), (2, 1), (3, 0), (3, 1)]
    mats = pieces[1:]

    @pl.when(jnp.logical_and(moved, odd == 1))
    def _():
        for k, h in pieces:
            fetch(k, h, wdst(k, r, h), True)

    @pl.when(jnp.logical_and(moved, odd == 0))
    def _():
        for k, h in pieces:
            fetch(k, h, sw(k, h), True)

    @pl.when(jnp.logical_and(jnp.logical_not(moved), home))
    def _():
        for k, h in pieces:
            fetch(k, h, wdst(k, r, h), False)

    @pl.when(jnp.logical_not(jnp.logical_or(moved, home)))
    def _():
        for k, h in pieces:
            fetch(k, h, sw(k, h), False)

    @pl.when(layer == 0)
    def _():
        for u in range(units):
            pltpu.make_async_copy(x_hbm.at[m, pl.ds(u * UNIT, UNIT)], xbuf.at[u], x0_sem.at[u]).start()

    kc, vt = (kc0, kc1, kc2, kc3), (vt0, vt1, vt2, vt3)
    for ref in kc + vt:
        ref[...] = jnp.zeros_like(ref)
    length = lens[m]
    key = lax.broadcasted_iota(jnp.int32, (seq, LANE), 0)
    lane = lax.broadcasted_iota(jnp.int32, (seq, LANE), 1)
    high = (key // KBLK) * KBLK
    part = jnp.where(lane % 2 == 0, high, key - high).astype(jnp.float32)
    dead = jnp.where(key >= length, NEG, 0.0)
    kx[...] = jnp.where(lane < 6, part, jnp.where(lane == 6, dead, 0.0)).astype(jnp.bfloat16)
    slopes = alibi_slopes(heads_n)
    row = lax.broadcasted_iota(jnp.int32, (LANE, KBLK), 0)
    second = lax.broadcasted_iota(jnp.int32, (LANE, KBLK), 1) >= LANE
    for pair in range(pairs):
        (h0, m0, l0), (h1, m1, l1) = split_bf16(slopes[2 * pair]), split_bf16(slopes[2 * pair + 1])
        hi, mid, low = jnp.where(second, h1, h0), jnp.where(second, m1, m0), jnp.where(second, l1, l0)
        val = jnp.where(row < 2, hi, jnp.where(row < 4, mid, jnp.where(row < 6, low, jnp.where(row == 6, 1.0, 0.0))))
        for side in range(2):
            qaug[pair, side, LANE:, :] = val[:, side * LANE:(side + 1) * LANE].astype(jnp.bfloat16)
    kpos = lax.broadcasted_iota(jnp.int32, (KBLK, KBLK), 0)
    qpos = lax.broadcasted_iota(jnp.int32, (KBLK, KBLK), 1) % LANE
    cmask[0] = jnp.where(kpos <= qpos, 0.0, NEG)
    cmask[1] = jnp.where(kpos <= qpos + LANE, 0.0, NEG)

    def to_relay(k, h):
        rcopy(wdst(k, r, h), rl(k, h), rl_send.at[h, k], rl_recv.at[h, k], tp=(rp, rm)[h]).start()

    def to_partner(k, q, d, h):
        rcopy(wdst(k, q, h), wdst(k, q, h), fwd_send.at[d, k, h], w_recv.at[d, k, h], pp=partner).start()

    def hand_out(behind=()):
        for i, (k, h) in enumerate(pieces):
            wwait(sw(k, h), sw_recv.at[k, h])
            rcopy(sw(k, h), wdst(k, r, h), dir_send.at[0, k, h], w_recv.at[3, k, h], tp=rp).start()
            rcopy(sw(k, h), wdst(k, r, h), dir_send.at[1, k, h], w_recv.at[1, k, h], tp=rm).start()
            if 3 <= i < len(behind) + 3:
                relay_weights(*behind[i - 3])

    def relay_weights(k, h):
        wwait(rl(k, h), rl_recv.at[h, k])
        rcopy(rl(k, h), wdst(k, (rm, rp)[h], h), rl_send.at[h, k], w_recv.at[2, k, h], tp=(rp, rm)[h]).start()

    def from_partner():
        for d, q in ((0, r), (1, rp), (3, rm), (2, ro)):
            for k, h in pieces:
                wwait(wdst(k, q, h), w_recv.at[d, k, h])

    def sent(view, sem):
        rcopy(view, view, sem, sem, pp=partner).wait_send()

    def handed_out():
        for k, h in pieces:
            for d in range(2):
                sent(sw(k, h), dir_send.at[d, k, h])
        for k, h in mats:
            sent(rl(k, h), rl_send.at[h, k])

    @pl.when(home)
    def _():
        for k, h in pieces:
            wwait(wdst(k, r, h), sw_recv.at[k, h])
            if k == 4:
                rcopy(wdst(k, r), wdst(k, r), pk_send.at[0], w_recv.at[2, k, h], tp=ro).start()
            else:
                @pl.when(ahead)
                def _():
                    to_relay(k, h)
            to_partner(k, r, 0, h)

        @pl.when(jnp.logical_not(ahead))
        def _():
            pl.semaphore_wait(go, 1)
            for k, h in mats:
                to_relay(k, h)

        for k, h in pieces:
            for d, q in ((1, rp), (3, rm)):
                wwait(wdst(k, q, h), w_recv.at[d, k, h])
                to_partner(k, q, d, h)
        for k, h in pieces:
            wwait(wdst(k, ro, h), w_recv.at[2, k, h])
            to_partner(k, ro, 2, h)

    late_source = jnp.logical_not(jnp.logical_or(home, jnp.logical_or(r % 2 == 1, level)))

    @pl.when(jnp.logical_not(jnp.logical_or(home, late_source)))
    def _():
        hand_out(mats)
        for k, h in mats[len(pieces) - 3:]:
            relay_weights(k, h)
        handed_out()

        @pl.when(jnp.logical_not(level))
        def _():
            pl.semaphore_signal(go, inc=1, device_id={"pp": partner}, device_id_type=MESH)

        from_partner()

    @pl.when(late_source)
    def _():
        hand_out()
        from_partner()

    def out_at(mm, u):
        return out.at[mm, pl.ds(pl.multiple_of(u * UNIT, UNIT), UNIT)]

    m_a = micro_of(rm, 0, stage1)
    m_b = micro_of(rp, 1, stage1)
    relay = jnp.logical_and(odd == 0, jnp.logical_or(c == 1, x % 2 == 0))
    lag = min(5, units) * (x % 2) + (1 - x % 2) * (min(5, units) + (units - min(5, units)) * (x // 2))
    hold = min(5, units) * (1 - (x + 2) // 3) + (x + 2) // 3

    def relay_unit(v):
        wwait(out_at(m_a, v), rr_recv.at[0, v])
        rcopy(out_at(m_a, v), out_at(m_a, v), rr_send.at[0, v], o_recv, tp=rp).start()
        wwait(out_at(m_b, v), rr_recv.at[1, v])
        rcopy(out_at(m_b, v), out_at(m_b, v), rr_send.at[1, v], o_recv, tp=rm).start()

    def wide(parts):
        return jnp.concatenate(parts, axis=1)

    def blocks(ref, first, count):
        return wide([ref[first + i] for i in range(count)])

    def put_blocks(ref, first, val):
        for i in range(val.shape[1] // LANE):
            ref[first + i] = val[:, i * LANE:(i + 1) * LANE]

    def attention(nb, diag, tok, u):
        head_row = lax.broadcasted_iota(jnp.int32, (LANE, LANE), 0) < 64

        def project(q):
            for j in range(3):
                weights = wide([wqkv[q, j * per_q + i] for i in range(per_q)])
                o = jnp.dot(blocks(abuf, 0, pairs), weights, preferred_element_type=jnp.float32)
                o = (o + packs[q, 7:8, j * quarter:(j + 1) * quarter]).astype(jnp.bfloat16)
                for i in range(per_q):
                    part = o[:, i * LANE:(i + 1) * LANE]
                    if j == 0:
                        q_t = (part.astype(jnp.float32) * 0.125).T
                        qaug[q * per_q + i, 0, :LANE, :] = jnp.where(head_row, q_t, 0.0).astype(jnp.bfloat16)
                        qaug[q * per_q + i, 1, :LANE, :] = jnp.where(head_row, 0.0, q_t).astype(jnp.bfloat16)
                    elif j == 1:
                        kc[q][i, tok, :] = part
                    else:
                        vt[q][i, u] = part.astype(jnp.float32).T.astype(jnp.bfloat16)

        def scores(pair):
            kq = kc[pair // per_q]
            q_rhs = blocks(qaug.at[pair], 0, 2)
            top = None
            for b in range(nb):
                keys = wide([kq[pair % per_q, b * KBLK:(b + 1) * KBLK, :], kx[b * KBLK:(b + 1) * KBLK, :]])
                s = jnp.dot(keys, q_rhs, preferred_element_type=jnp.float32)
                if b == nb - 1:
                    s = s + diag
                sbuf[pair % 2, b] = s
                peak = jnp.max(s, axis=0, keepdims=True)
                top = peak if top is None else jnp.maximum(top, peak)
            return top

        def weigh(pair, top):
            vq = vt[pair // per_q].at[pair % per_q]
            total = None
            acc = None
            for b in range(nb):
                e = jnp.exp(sbuf[pair % 2, b] - top)
                part_sum = jnp.sum(e, axis=0, keepdims=True)
                total = part_sum if total is None else total + part_sum
                pv = jnp.dot(blocks(vq, b * KBLK // UNIT, KBLK // UNIT), e.astype(jnp.bfloat16), preferred_element_type=jnp.float32)
                acc = pv if acc is None else acc + pv
            acc = acc * (1.0 / total)
            both = jnp.concatenate([acc[:64, :LANE], acc[64:, LANE:]], axis=0)
            ctx[pair] = both.T.astype(jnp.bfloat16)

        project(0)
        top = None
        for pair in range(pairs + 1):
            if pair % per_q == 0 and pair // per_q + 1 < tp_n:
                project(pair // per_q + 1)
            later = scores(pair) if pair < pairs else None
            if pair > 0:
                weigh(pair - 1, top)
            top = later

    more = layer < 2 * x_n - 1
    nxt = (layer + 1) % (2 * x_n)
    half_n = nxt // 2
    x_next = half_n + (1 - nxt % 2) * (1 - half_n % 2) * (2 - 2 * half_n)
    p_next = 2 * x_next + c
    r_next = (r + (1 - odd) * (x % 2) * sig + tp_n) % tp_n

    def store_input(v):
        @pl.when(odd == 1)
        def _():
            @pl.when(c == 0)
            def _():
                pltpu.make_async_copy(xbuf.at[v], out_at(m, v), o_recv).start()

            @pl.when(c == 1)
            def _():
                rcopy(xbuf.at[v], out_at(m, v), fa_send.at[v], o_recv, pp=partner).start()

            @pl.when(x % 2 == 1)
            def _():
                rcopy(xbuf.at[v], out_at(m, v), fb_send.at[v], o_recv, tp=r_fwd, pp=stage0).start()

            @pl.when(x % 2 == 0)
            def _():
                rcopy(xbuf.at[v], out_at(m, v), fb_send.at[v], rr_recv.at[c, v], tp=r_fwd, pp=stage0).start()
                rcopy(xbuf.at[v], out_at(m, v), fc_send.at[v], o_recv, tp=r_bwd, pp=stage0).start()

    def store_unit(v, cols=slice(None)):
        src, dst = ybuf.at[v, :, cols], out.at[m, pl.ds(pl.multiple_of(v * UNIT, UNIT), UNIT), cols]

        @pl.when(odd == 1)
        def _():
            rcopy(src, dst, db_send.at[v], rr_recv.at[c, v], tp=r_fwd, pp=stage1).start()

        rcopy(src, dst, da_send.at[v], o_recv, tp=r_bwd, pp=2 * x + odd).start()

        @pl.when(home)
        def _():
            pltpu.make_async_copy(src, dst, o_recv).start()

        @pl.when(jnp.logical_not(home))
        def _():
            rcopy(src, dst, od_send.at[v], o_recv, pp=partner).start()

    stores = jnp.logical_or(odd == 1, x % 2 == 1)
    stores_later = jnp.logical_and(stores, more)

    def unit_step(u, carry):
        tok = pl.ds(pl.multiple_of(u * UNIT, UNIT), UNIT)

        for group, (step0, step1) in (((0, 1), (2, 0)), ((2,), (4, 1)), ((3,), (6, 2))):
            now = jnp.logical_or(jnp.logical_and(layer == 0, u == min(step0, units - 1)),
                                 jnp.logical_or(jnp.logical_and(layer == 1, u == min(step1, units - 1)), jnp.logical_and(layer > 1, u == 0)))

            @pl.when(jnp.logical_and(late_source, now))
            def _():
                for k in group:
                    for h in range(2):
                        relay_weights(k, h)

        @pl.when(jnp.logical_and(relay, u >= lag))
        def _():
            relay_unit(u - lag)

        @pl.when(layer == 0)
        def _():
            pltpu.make_async_copy(x_hbm.at[m, tok], xbuf.at[u], x0_sem.at[u]).wait()

        @pl.when(layer > 0)
        def _():
            wwait(xbuf.at[u], x_recv.at[u])

        @pl.when(jnp.logical_and(stores, u >= hold - 1))
        def _():
            store_input(u - hold + 1)

        @pl.when(jnp.logical_and(stores_later, u >= hold))
        def _():
            store_unit(u - hold)

        xin = xbuf[u].astype(jnp.float32)
        put_blocks(abuf, 0, layer_norm(xin, packs[0, 0:1, :], packs[0, 1:2, :]))
        for nb in range(1, seq // KBLK + 1):
            @pl.when(u // 2 + 1 == nb)
            def _():
                attention(nb, cmask[u % 2], tok, u)

        for n in range(model // KBLK):
            cols = slice(n * KBLK, (n + 1) * KBLK)
            attn = jnp.dot(blocks(ctx, 0, pairs), blocks(wout, 2 * n, 2), preferred_element_type=jnp.float32)
            hbuf[:, cols] = (xbuf[u, :, cols].astype(jnp.float32) + attn + packs[0, 2:3, cols]).astype(jnp.bfloat16)
        put_blocks(abuf, 0, layer_norm(hbuf[...].astype(jnp.float32), packs[0, 3:4, :], packs[0, 4:5, :]))
        for q in range(tp_n):
            for n in range(hid_q // KBLK):
                up = jnp.dot(blocks(abuf, 0, pairs), blocks(wup.at[q], 2 * n, 2), preferred_element_type=jnp.float32)
                up = up + packs[q, 6:7, n * KBLK:(n + 1) * KBLK]
                put_blocks(ubuf, q * (hid_q // LANE) + 2 * n, gelu(up).astype(jnp.bfloat16))
        half_model = model // 2
        for n in range(2):
            cols = slice(n * half_model, (n + 1) * half_model)
            down = jnp.dot(blocks(ubuf, 0, ubuf.shape[0]), blocks(wdn, n * (half_model // LANE), half_model // LANE), preferred_element_type=jnp.float32)
            ybuf[u, :, cols] = (hbuf[:, cols].astype(jnp.float32) + down + packs[0, 5:6, cols]).astype(jnp.bfloat16)

            @pl.when(more)
            def _():
                rcopy(ybuf.at[u, :, cols], xbuf.at[u, :, cols], s_send.at[u], x_recv.at[u], tp=r_next, pp=p_next).start()

            @pl.when(jnp.logical_not(more))
            def _():
                store_unit(u, cols)

        return carry

    lax.fori_loop(0, units, unit_step, 0)

    @pl.when(stores_later)
    def _():
        def last(v, carry):
            store_unit(v)
            return carry

        lax.fori_loop(units - hold, units, last, 0)

    @pl.when(stores)
    def _():
        def last_input(v, carry):
            store_input(v)
            return carry

        lax.fori_loop(units - hold + 1, units, last_input, 0)

    @pl.when(relay)
    def _():
        def rest(v, carry):
            relay_unit(v)
            return carry

        lax.fori_loop(units - lag, units, rest, 0)

    @pl.when(moved)
    def _():
        for k, h in pieces:
            sent(sw(k, h), sw_send.at[k, h])

    @pl.when(home)
    def _():
        sent(sw_pack, pk_send.at[0])
        for k, h in mats:
            sent(rl(k, h), rl_send.at[h, k])
        for d in range(4):
            for k, h in pieces:
                sent(sw(k, h), fwd_send.at[d, k, h])

    @pl.when(late_source)
    def _():
        handed_out()

    def drain(u, carry):
        @pl.when(more)
        def _():
            sent(ybuf.at[u], s_send.at[u])

        @pl.when(stores)
        def _():
            sent(ybuf.at[u], da_send.at[u])

            @pl.when(jnp.logical_not(home))
            def _():
                sent(ybuf.at[u], od_send.at[u])

        @pl.when(relay)
        def _():
            sent(ybuf.at[u], rr_send.at[0, u])
            sent(ybuf.at[u], rr_send.at[1, u])

        @pl.when(odd == 1)
        def _():
            sent(ybuf.at[u], db_send.at[u])
            sent(ybuf.at[u], fb_send.at[u])

            @pl.when(x % 2 == 0)
            def _():
                sent(ybuf.at[u], fc_send.at[u])

            @pl.when(c == 1)
            def _():
                sent(ybuf.at[u], fa_send.at[u])

        return carry

    lax.fori_loop(0, units, drain, 0)

    @pl.when(relay)
    def _():
        wwait(out.at[pl.ds(0, out.shape[0] // 2)], o_recv)

    @pl.when(jnp.logical_not(relay))
    def _():
        wwait(out, o_recv)


def solution(mesh):
    tp_size = mesh.shape['tp']
    in_specs = (P('dp'), P('dp'), P('pp'), P('pp'), P('pp', None, None, 'tp'), P('pp', None, 'tp', None), P('pp', 'tp', None), P('pp'), P('pp'), P('pp'), P('pp', None, 'tp'), P('pp', 'tp'), P('pp', 'tp', None), P('pp'))

    def per_device(x_in, seq_lens, ln1_gain, ln1_shift, w_qkv, b_qkv, w_out, b_out, ln2_gain, ln2_shift, w_up, b_up, w_down, b_down):
        micro_n, batch_n, seq_n, model_n = x_in.shape
        heads_n = b_qkv.shape[2] * tp_size
        quarter = w_qkv.shape[3]
        hid_q = w_up.shape[2]
        bf16, f32 = jnp.bfloat16, jnp.float32
        wqkv_t = jnp.transpose(w_qkv[0], (1, 0, 2))
        vectors = (ln1_gain, ln1_shift, b_out, ln2_gain, ln2_shift, b_down, b_up, b_qkv)
        pack_shape = (len(vectors), model_n)
        units = seq_n // UNIT
        pairs = model_n // LANE
        dma = pltpu.SemaphoreType.DMA
        anywhere = pl.BlockSpec(memory_space=pl.ANY)
        tokens = batch_n * seq_n
        out = pl.pallas_call(
            functools.partial(kernel, heads_n),
            out_shape=jax.ShapeDtypeStruct((micro_n, tokens, model_n), bf16),
            in_specs=[anywhere, pl.BlockSpec(memory_space=pltpu.SMEM)] + [anywhere] * 4 + [pl.BlockSpec(memory_space=pltpu.VMEM)] * len(vectors),
            out_specs=anywhere,
            scratch_shapes=[
                pltpu.VMEM((tp_size, 3 * quarter // LANE, model_n, LANE), bf16),
                pltpu.VMEM((model_n // LANE, tp_size * quarter, LANE), bf16),
                pltpu.VMEM((tp_size, hid_q // LANE, model_n, LANE), bf16),
                pltpu.VMEM((model_n // LANE, tp_size * hid_q, LANE), bf16),
                pltpu.VMEM((tp_size,) + pack_shape, f32),
                pltpu.VMEM(pack_shape, f32),
                pltpu.VMEM((2, 3 * quarter // LANE, model_n // 2, LANE), bf16),
                pltpu.VMEM((2, model_n // LANE, quarter // 2, LANE), bf16),
                pltpu.VMEM((2, hid_q // LANE, model_n // 2, LANE), bf16),
                pltpu.VMEM((2, model_n // LANE, hid_q // 2, LANE), bf16),
                pltpu.VMEM((3 * quarter // LANE, model_n, LANE), bf16),
                pltpu.VMEM((model_n // LANE, quarter, LANE), bf16),
                pltpu.VMEM((hid_q // LANE, model_n, LANE), bf16),
                pltpu.VMEM((model_n // LANE, hid_q, LANE), bf16),
                pltpu.VMEM(pack_shape, f32),
                pltpu.VMEM((units, UNIT, model_n), bf16),
                pltpu.VMEM((units, UNIT, model_n), bf16),
                *[pltpu.VMEM((quarter // LANE, seq_n, LANE), bf16)] * tp_size,
                *[pltpu.VMEM((quarter // LANE, units, LANE, UNIT), bf16)] * tp_size,
                pltpu.VMEM((seq_n, LANE), bf16),
                pltpu.VMEM((pairs, 2, KBLK, LANE), bf16),
                pltpu.VMEM((2, KBLK, KBLK), f32),
                pltpu.VMEM((2, seq_n // KBLK, KBLK, KBLK), f32),
                pltpu.VMEM((model_n // LANE, UNIT, LANE), bf16),
                pltpu.VMEM((model_n // LANE, UNIT, LANE), bf16),
                pltpu.VMEM((UNIT, model_n), bf16),
                pltpu.VMEM((tp_size * hid_q // LANE, UNIT, LANE), bf16),
                dma((5, 2)), dma((5, 2)), dma((4, 5, 2)), dma((4, 5, 2)), dma((2, 4)), dma((2, 4)), dma((2, 5, 2)), dma((1,)), pltpu.SemaphoreType.REGULAR,
                *[dma((units,))] * 9,
                dma((2, units)), dma((2, units)), dma,
            ],
            compiler_params=pltpu.CompilerParams(collective_id=0, has_side_effects=True, vmem_limit_bytes=63 * 1024 * 1024),
            cost_estimate=pl.CostEstimate(flops=30 * 10 ** 9, bytes_accessed=40 * 10 ** 6, transcendentals=10 ** 7),
        )(x_in.reshape(micro_n, tokens, model_n), seq_lens.reshape(micro_n * batch_n), wqkv_t, w_out[0], w_up[0], w_down[0], *vectors)
        return out.reshape((1,) + x_in.shape)

    return jax.shard_map(per_device, mesh=mesh, in_specs=in_specs, out_specs=P('pp', 'dp'), check_vma=False)
```

profile of v0, /device:TPU:103, one launch (start us, length us, event | category | flops | bytes accessed | tf_op | source)
XLA Modules:
  0.0 292.2 jit_solution(16153532496530058322)
XLA Ops:
  0.0 284.4 %shard_map.136 = bf16[4,1024,1024]{2,1,0:T(8,128)(2,1)} custom-call(bf16[4,1024,1024]{2,1,0:T(8,128)(2,1)} %bitcast.12, s32[4]{0:T(128)} %bitcast.17, bf16[3,1024,256]{2,1,0:T(8,128)(2,1)} %bitcast.15, bf16[256,1024]{1,0:T(8,128)(2,1)} %bitcast.16, bf16[1024,1024]{1,0:T(8,128)(2,1)} %bitcast.13, bf16[1024,1024]{1,0:T(8,128)(2,1)} %bitcast.14, ...), custom_call_target="tpu_custom_call" | custom-call | flops 30000001024 | bytes 40000000 | tf_op jit(solution)/shard_map/pallas_call | solution.py:583
  284.5 7.8 %copy.17 = bf16[1,4,1,1024,1024]{4,3,2,1,0:T(8,128)(2,1)} copy(bf16[1,4,1,1024,1024]{4,3,2,1,0:T(8,128)(2,1)} %bitcast.11) | data formatting | bytes 16777216
where the time goes:
time: 292 us
  Pallas kernels  284 us (97%)
  local copies, waits for them, and re-layouts  7.76 us (3%)
    pallas_call x1, Pallas kernels, per_device(): pl.pallas_call(functools.partial(kernel, heads_n), out_shape=jax.ShapeDty...  284 us
    unnamed x1, local copies, waits for them, and re-layouts  7.76 us

commit v1 on v0

--- a/solution.py
+++ b/solution.py
@@ -279,8 +279,12 @@
         hand_out()
         from_partner()
 
-    def out_at(mm, u):
-        return out.at[mm, pl.ds(pl.multiple_of(u * UNIT, UNIT), UNIT)]
+    def half_cols(half):
+        return slice(half * (model // 2), (half + 1) * (model // 2))
+
+    def out_at(mm, u, half=None):
+        rows = pl.ds(pl.multiple_of(u * UNIT, UNIT), UNIT)
+        return out.at[mm, rows] if half is None else out.at[mm, rows, half_cols(half)]
 
     m_a = micro_of(rm, 0, stage1)
     m_b = micro_of(rp, 1, stage1)
@@ -289,10 +293,11 @@
     hold = min(5, units) * (1 - (x + 2) // 3) + (x + 2) // 3
 
     def relay_unit(v):
-        wwait(out_at(m_a, v), rr_recv.at[0, v])
-        rcopy(out_at(m_a, v), out_at(m_a, v), rr_send.at[0, v], o_recv, tp=rp).start()
-        wwait(out_at(m_b, v), rr_recv.at[1, v])
-        rcopy(out_at(m_b, v), out_at(m_b, v), rr_send.at[1, v], o_recv, tp=rm).start()
+        for half in range(2):
+            for slot, (mm, to) in enumerate(((m_a, rp), (m_b, rm))):
+                part = out_at(mm, v, half)
+                wwait(part, rr_recv.at[slot, v, half])
+                rcopy(part, part, rr_send.at[slot, v], o_recv, tp=to).start()
 
     def wide(parts):
         return jnp.concatenate(parts, axis=1)
@@ -385,15 +390,16 @@
 
             @pl.when(x % 2 == 0)
             def _():
-                rcopy(xbuf.at[v], out_at(m, v), fb_send.at[v], rr_recv.at[c, v], tp=r_fwd, pp=stage0).start()
+                for half in range(2):
+                    rcopy(xbuf.at[v, :, half_cols(half)], out_at(m, v, half), fb_send.at[v], rr_recv.at[c, v, half], tp=r_fwd, pp=stage0).start()
                 rcopy(xbuf.at[v], out_at(m, v), fc_send.at[v], o_recv, tp=r_bwd, pp=stage0).start()
 
-    def store_unit(v, cols=slice(None)):
-        src, dst = ybuf.at[v, :, cols], out.at[m, pl.ds(pl.multiple_of(v * UNIT, UNIT), UNIT), cols]
+    def store_half(v, half):
+        src, dst = ybuf.at[v, :, half_cols(half)], out_at(m, v, half)
 
         @pl.when(odd == 1)
         def _():
-            rcopy(src, dst, db_send.at[v], rr_recv.at[c, v], tp=r_fwd, pp=stage1).start()
+            rcopy(src, dst, db_send.at[v], rr_recv.at[c, v, half], tp=r_fwd, pp=stage1).start()
 
         rcopy(src, dst, da_send.at[v], o_recv, tp=r_bwd, pp=2 * x + odd).start()
 
@@ -404,6 +410,10 @@
         @pl.when(jnp.logical_not(home))
         def _():
             rcopy(src, dst, od_send.at[v], o_recv, pp=partner).start()
+
+    def store_unit(v):
+        store_half(v, 0)
+        store_half(v, 1)
 
     stores = jnp.logical_or(odd == 1, x % 2 == 1)
     stores_later = jnp.logical_and(stores, more)
@@ -470,7 +480,7 @@
 
             @pl.when(jnp.logical_not(more))
             def _():
-                store_unit(u, cols)
+                store_half(u, n)
 
         return carry
 
@@ -615,7 +625,7 @@
                 pltpu.VMEM((tp_size * hid_q // LANE, UNIT, LANE), bf16),
                 dma((5, 2)), dma((5, 2)), dma((4, 5, 2)), dma((4, 5, 2)), dma((2, 4)), dma((2, 4)), dma((2, 5, 2)), dma((1,)), pltpu.SemaphoreType.REGULAR,
                 *[dma((units,))] * 9,
-                dma((2, units)), dma((2, units)), dma,
+                dma((2, units, 2)), dma((2, units)), dma,
             ],
             compiler_params=pltpu.CompilerParams(collective_id=0, has_side_effects=True, vmem_limit_bytes=63 * 1024 * 1024),
             cost_estimate=pl.CostEstimate(flops=30 * 10 ** 9, bytes_accessed=40 * 10 ** 6, transcendentals=10 ** 7),

time: 292 us -> 291 us (level)
  no operation moved by 1% of the time
where the time goes in v1:
time: 291 us; the launch traced here: 290 us
  Pallas kernels  283 us (97%)
  local copies, waits for them, and re-layouts  7.76 us (3%)
    pallas_call x1, Pallas kernels, per_device(): pl.pallas_call(functools.partial(kernel, heads_n), out_shape=jax.ShapeDty...  283 us
    unnamed x1, local copies, waits for them, and re-layouts  7.76 us

profile of v1, /device:TPU:103, one launch (start us, length us, event | category | flops | bytes accessed | tf_op | source)
XLA Modules:
  0.0 290.4 jit_solution(4423677857511667828)
XLA Ops:
  0.0 282.6 %shard_map.136 = bf16[4,1024,1024]{2,1,0:T(8,128)(2,1)} custom-call(bf16[4,1024,1024]{2,1,0:T(8,128)(2,1)} %bitcast.12, s32[4]{0:T(128)} %bitcast.17, bf16[3,1024,256]{2,1,0:T(8,128)(2,1)} %bitcast.15, bf16[256,1024]{1,0:T(8,128)(2,1)} %bitcast.16, bf16[1024,1024]{1,0:T(8,128)(2,1)} %bitcast.13, bf16[1024,1024]{1,0:T(8,128)(2,1)} %bitcast.14, ...), custom_call_target="tpu_custom_call" | custom-call | flops 30000001024 | bytes 40000000 | tf_op jit(solution)/shard_map/pallas_call | solution.py:593
  282.6 7.8 %copy.17 = bf16[1,4,1,1024,1024]{4,3,2,1,0:T(8,128)(2,1)} copy(bf16[1,4,1,1024,1024]{4,3,2,1,0:T(8,128)(2,1)} %bitcast.11) | data formatting | bytes 16777216

commit v2 on v1

--- a/solution.py
+++ b/solution.py
@@ -251,13 +251,15 @@
             for k, h in mats:
                 to_relay(k, h)
 
-        for k, h in pieces:
-            for d, q in ((1, rp), (3, rm)):
-                wwait(wdst(k, q, h), w_recv.at[d, k, h])
-                to_partner(k, q, d, h)
-        for k, h in pieces:
-            wwait(wdst(k, ro, h), w_recv.at[2, k, h])
-            to_partner(k, ro, 2, h)
+        for i, (k, h) in enumerate(pieces + mats[:2]):
+            if i < len(pieces):
+                for d, q in ((1, rp), (3, rm)):
+                    wwait(wdst(k, q, h), w_recv.at[d, k, h])
+                    to_partner(k, q, d, h)
+            if i >= 2:
+                k, h = pieces[i - 2]
+                wwait(wdst(k, ro, h), w_recv.at[2, k, h])
+                to_partner(k, ro, 2, h)
 
     late_source = jnp.logical_not(jnp.logical_or(home, jnp.logical_or(r % 2 == 1, level)))
 
@@ -421,7 +423,7 @@
     def unit_step(u, carry):
         tok = pl.ds(pl.multiple_of(u * UNIT, UNIT), UNIT)
 
-        for group, (step0, step1) in (((0, 1), (2, 0)), ((2,), (4, 1)), ((3,), (6, 2))):
+        for group, (step0, step1) in (((0, 1), (3, 0)), ((2,), (5, 1)), ((3,), (7, 2))):
             now = jnp.logical_or(jnp.logical_and(layer == 0, u == min(step0, units - 1)),
                                  jnp.logical_or(jnp.logical_and(layer == 1, u == min(step1, units - 1)), jnp.logical_and(layer > 1, u == 0)))
 

time: 291 us -> 294 us (1.010)
  Pallas kernels: 283 us -> 286 us
    pallas_call x1, Pallas kernels: 283 us -> 286 us  [per_device(): pl.pallas_call(functools.partial(kernel, heads_n), out_shape=jax.ShapeDty...]
where the time goes in v2:
time: 294 us
  Pallas kernels  286 us (97%)
  local copies, waits for them, and re-layouts  7.76 us (3%)
    pallas_call x1, Pallas kernels, per_device(): pl.pallas_call(functools.partial(kernel, heads_n), out_shape=jax.ShapeDty...  286 us
    unnamed x1, local copies, waits for them, and re-layouts  7.76 us

profile of v2, /device:TPU:103, one launch (start us, length us, event | category | flops | bytes accessed | tf_op | source)
XLA Modules:
  0.0 293.6 jit_solution(7258581014188607616)
XLA Ops:
  0.0 285.8 %shard_map.136 = bf16[4,1024,1024]{2,1,0:T(8,128)(2,1)} custom-call(bf16[4,1024,1024]{2,1,0:T(8,128)(2,1)} %bitcast.12, s32[4]{0:T(128)} %bitcast.17, bf16[3,1024,256]{2,1,0:T(8,128)(2,1)} %bitcast.15, bf16[256,1024]{1,0:T(8,128)(2,1)} %bitcast.16, bf16[1024,1024]{1,0:T(8,128)(2,1)} %bitcast.13, bf16[1024,1024]{1,0:T(8,128)(2,1)} %bitcast.14, ...), custom_call_target="tpu_custom_call" | custom-call | flops 30000001024 | bytes 40000000 | tf_op jit(solution)/shard_map/pallas_call | solution.py:595
  285.8 7.8 %copy.17 = bf16[1,4,1,1024,1024]{4,3,2,1,0:T(8,128)(2,1)} copy(bf16[1,4,1,1024,1024]{4,3,2,1,0:T(8,128)(2,1)} %bitcast.11) | data formatting | bytes 16777216

commit v3 on v2

--- a/solution.py
+++ b/solution.py
@@ -423,7 +423,7 @@
     def unit_step(u, carry):
         tok = pl.ds(pl.multiple_of(u * UNIT, UNIT), UNIT)
 
-        for group, (step0, step1) in (((0, 1), (3, 0)), ((2,), (5, 1)), ((3,), (7, 2))):
+        for group, (step0, step1) in (((0, 1), (2, 0)), ((2,), (3, 1)), ((3,), (5, 2))):
             now = jnp.logical_or(jnp.logical_and(layer == 0, u == min(step0, units - 1)),
                                  jnp.logical_or(jnp.logical_and(layer == 1, u == min(step1, units - 1)), jnp.logical_and(layer > 1, u == 0)))
 

time: 294 us -> 290 us (0.986)
  Pallas kernels: 286 us -> 282 us
    pallas_call x1, Pallas kernels: 286 us -> 282 us  [per_device(): pl.pallas_call(functools.partial(kernel, heads_n), out_shape=jax.ShapeDty...]
where the time goes in v3:
time: 290 us
  Pallas kernels  282 us (97%)
  local copies, waits for them, and re-layouts  7.76 us (3%)
    pallas_call x1, Pallas kernels, per_device(): pl.pallas_call(functools.partial(kernel, heads_n), out_shape=jax.ShapeDty...  282 us
    unnamed x1, local copies, waits for them, and re-layouts  7.76 us

profile of v3, /device:TPU:103, one launch (start us, length us, event | category | flops | bytes accessed | tf_op | source)
XLA Modules:
  0.0 289.8 jit_solution(16382557380108612019)
XLA Ops:
  0.0 282.1 %shard_map.136 = bf16[4,1024,1024]{2,1,0:T(8,128)(2,1)} custom-call(bf16[4,1024,1024]{2,1,0:T(8,128)(2,1)} %bitcast.12, s32[4]{0:T(128)} %bitcast.17, bf16[3,1024,256]{2,1,0:T(8,128)(2,1)} %bitcast.15, bf16[256,1024]{1,0:T(8,128)(2,1)} %bitcast.16, bf16[1024,1024]{1,0:T(8,128)(2,1)} %bitcast.13, bf16[1024,1024]{1,0:T(8,128)(2,1)} %bitcast.14, ...), custom_call_target="tpu_custom_call" | custom-call | flops 30000001024 | bytes 40000000 | tf_op jit(solution)/shard_map/pallas_call | solution.py:595
  282.1 7.8 %copy.17 = bf16[1,4,1,1024,1024]{4,3,2,1,0:T(8,128)(2,1)} copy(bf16[1,4,1,1024,1024]{4,3,2,1,0:T(8,128)(2,1)} %bitcast.11) | data formatting | bytes 16777216

commit v4 on v3

--- a/solution.py
+++ b/solution.py
@@ -107,7 +107,6 @@
         for head in range(quarter // width):
             at = j * quarter + head * width
             pack_in[7:8, at:at + width] = b_qkv[0, j, head:head + 1, :].astype(jnp.float32)
-    pl.semaphore_wait(barrier, 10)
 
     def wsrc(k, h, n):
         if k == 0:
@@ -151,6 +150,18 @@
     pieces = [(4, 0), (1, 0), (1, 1), (0, 0), (0, 1), (2, 0), (2, 1), (3, 0), (3, 1)]
     mats = pieces[1:]
 
+    @pl.when(jnp.logical_and(jnp.logical_not(moved), home))
+    def _():
+        for k, h in pieces:
+            fetch(k, h, wdst(k, r, h), False)
+
+    @pl.when(jnp.logical_not(jnp.logical_or(moved, home)))
+    def _():
+        for k, h in pieces:
+            fetch(k, h, sw(k, h), False)
+
+    pl.semaphore_wait(barrier, 10)
+
     @pl.when(jnp.logical_and(moved, odd == 1))
     def _():
         for k, h in pieces:
@@ -160,16 +171,6 @@
     def _():
         for k, h in pieces:
             fetch(k, h, sw(k, h), True)
-
-    @pl.when(jnp.logical_and(jnp.logical_not(moved), home))
-    def _():
-        for k, h in pieces:
-            fetch(k, h, wdst(k, r, h), False)
-
-    @pl.when(jnp.logical_not(jnp.logical_or(moved, home)))
-    def _():
-        for k, h in pieces:
-            fetch(k, h, sw(k, h), False)
 
     @pl.when(layer == 0)
     def _():

time: 290 us -> 290 us (level)
  no operation moved by 1% of the time
where the time goes in v4:
time: 290 us
  Pallas kernels  282 us (97%)
  local copies, waits for them, and re-layouts  7.76 us (3%)
    pallas_call x1, Pallas kernels, per_device(): pl.pallas_call(functools.partial(kernel, heads_n), out_shape=jax.ShapeDty...  282 us
    unnamed x1, local copies, waits for them, and re-layouts  7.76 us

profile of v4, /device:TPU:103, one launch (start us, length us, event | category | flops | bytes accessed | tf_op | source)
XLA Modules:
  0.0 290.2 jit_solution(15113251533578463939)
XLA Ops:
  0.0 282.5 %shard_map.136 = bf16[4,1024,1024]{2,1,0:T(8,128)(2,1)} custom-call(bf16[4,1024,1024]{2,1,0:T(8,128)(2,1)} %bitcast.12, s32[4]{0:T(128)} %bitcast.17, bf16[3,1024,256]{2,1,0:T(8,128)(2,1)} %bitcast.15, bf16[256,1024]{1,0:T(8,128)(2,1)} %bitcast.16, bf16[1024,1024]{1,0:T(8,128)(2,1)} %bitcast.13, bf16[1024,1024]{1,0:T(8,128)(2,1)} %bitcast.14, ...), custom_call_target="tpu_custom_call" | custom-call | flops 30000001024 | bytes 40000000 | tf_op jit(solution)/shard_map/pallas_call | solution.py:596
  282.5 7.8 %copy.17 = bf16[1,4,1,1024,1024]{4,3,2,1,0:T(8,128)(2,1)} copy(bf16[1,4,1,1024,1024]{4,3,2,1,0:T(8,128)(2,1)} %bitcast.11) | data formatting | bytes 16777216
